TPU v7x, 32 devices: a whole 2x2x4 slice. The times are simulated.
32 devices in a mesh: user: 16 (over z, y, x), seq: 2 (over core).
Axes of the slice: x: 2, y: 2, z: 4, core: 2. Of those that a mesh axis runs over, the one named last changes fastest.
Arguments:
- behaviors: bfloat16 [32, 2048, 256], P('user', 'seq'), may hold values from -20 to 20
- candidates: bfloat16 [32, 64, 256], P('user', 'seq'), may hold values from -64 to 64
- ranks: int32 [32, 2, 128], P('user', 'seq'), may hold values from 0 to 1151, as said below
- lengths: int32 [32], P('user'), may hold values from 1024 to 2048
- hash_planes: bfloat16 [256, 64], replicated, may hold values from -0.375 to 0.375
- norm_gain: float32 [256], replicated, may hold values from 0.5 to 1.5
- norm_bias: float32 [256], replicated, may hold values from -3 to 3
Outputs:
- interest: bfloat16 [32, 64, 256], P('user', 'seq')
Inputs may be any that keep to these rules, and one draw needn't show every extreme that they name: ranks[u, s, :] are 128 distinct positions of group s's window of 1152 behaviors; on the first group all are 128 or more.
All inputs are finite; a program needn't handle non-finite values.
Results may differ from a plain program's by a relative error of at most 0.0023.
Values may be sent and summed in bfloat16 or wider, within the bound.
No kernel may reach another device: no remote copies, remote signals or barrier semaphores. Data moves between devices by JAX's collectives and lax.ppermute only.
A program may use at most 64 MiB of HBM per device.

v0:
```python
import math
import jax
import jax.numpy as jnp
from jax import lax
from jax.sharding import PartitionSpec as P

HALO = 128
NEG_FILL = -1e30
HASH_WEIGHT = 2.0
NORM_EPS = 1e-05


def passed_along(value, axis, steps):
    count = lax.axis_size(axis)
    first, last = (max(0, -steps), min(count, count - steps))
    return lax.ppermute(value, axis, [(source, source + steps) for source in range(first, last)])


def joined(shard, axis, combine):
    everything = jax.tree.map(lambda part: lax.all_gather(part, axis), shard)
    first = jax.tree.map(lambda part: part[0], everything)

    def turn(k, so_far):
        return combine(so_far, jax.tree.map(lambda part: part[k], everything))

    return lax.fori_loop(1, lax.axis_size(axis), turn, first)


def soft_codes(rows, hash_planes):
    return jnp.tanh(jnp.dot(rows, hash_planes, preferred_element_type=jnp.float32)).astype(
        jnp.bfloat16
    )


def combine_parts(left_part, right_part):
    joint_max = jnp.maximum(left_part[0], right_part[0])
    left_scale = jnp.exp(left_part[0] - joint_max)
    right_scale = jnp.exp(right_part[0] - joint_max)
    total_sum = left_part[1] * left_scale + right_part[1] * right_scale
    vector_sum = left_part[2] * left_scale[..., None] + right_part[2] * right_scale[..., None]
    return (joint_max, total_sum, vector_sum)


def shards(behaviors, candidates, ranks, lengths, hash_planes, norm_gain, norm_bias):
    group_rows = behaviors.shape[1]
    feature_width = behaviors.shape[2]
    own_cands = candidates.shape[1]
    code_bits = hash_planes.shape[1]
    seq_index = lax.axis_index("seq")
    tail_rows = behaviors[:, group_rows - HALO :, :]
    before = passed_along(tail_rows, "seq", 1)
    queries = lax.all_gather(candidates, "seq", axis=1, tiled=True)
    window_pos = ranks[:, 0, :]
    from_tail = window_pos < HALO
    tail_index = jnp.clip(window_pos, 0, HALO - 1)
    own_index = jnp.clip(window_pos - HALO, 0, group_rows - 1)
    take_rows = jax.vmap(lambda row_table, where_at: row_table[where_at])
    picked = jnp.where(
        from_tail[:, :, None], take_rows(before, tail_index), take_rows(behaviors, own_index)
    )
    position = seq_index * group_rows - HALO + window_pos
    usable = (position >= 0) & (position < lengths[:, None])
    query_codes = soft_codes(queries, hash_planes)
    picked_codes = soft_codes(picked, hash_planes)
    similar = jnp.einsum("ucd,ukd->uck", queries, picked, preferred_element_type=jnp.float32)
    agreement = jnp.einsum(
        "ucb,ukb->uck", query_codes, picked_codes, preferred_element_type=jnp.float32
    )
    scores = similar * (1.0 / math.sqrt(feature_width)) + HASH_WEIGHT / code_bits * agreement
    usable_rows = usable[:, None, :]
    group_max = jnp.max(jnp.where(usable_rows, scores, NEG_FILL), axis=2)
    weights = jnp.where(usable_rows, jnp.exp(scores - group_max[..., None]), 0.0)
    group_total = jnp.sum(weights, axis=2)
    group_sum = jnp.einsum(
        "uck,ukd->ucd", weights.astype(jnp.bfloat16), picked, preferred_element_type=jnp.float32
    )
    merged = joined((group_max, group_total, group_sum), "seq", combine_parts)
    denominator = lax.dynamic_slice_in_dim(merged[1], seq_index * own_cands, own_cands, 1)
    numerator = lax.dynamic_slice_in_dim(merged[2], seq_index * own_cands, own_cands, 1)
    attended = numerator / denominator[..., None]
    moments = lax.psum(
        (jnp.sum(attended, axis=(0, 1)), jnp.sum(attended * attended, axis=(0, 1))), ("user", "seq")
    )
    row_count = attended.shape[0] * own_cands * lax.axis_size("user") * lax.axis_size("seq")
    feature_mean = moments[0] / row_count
    feature_var = moments[1] / row_count - feature_mean * feature_mean
    normed = (attended - feature_mean) * lax.rsqrt(feature_var + NORM_EPS) * norm_gain + norm_bias
    return normed.astype(jnp.bfloat16)


def solution(mesh):
    in_specs = (
        P("user", "seq", None),
        P("user", "seq", None),
        P("user", "seq", None),
        P("user"),
        P(),
        P(),
        P(),
    )
    out_specs = P("user", "seq", None)
    return jax.shard_map(shards, mesh=mesh, in_specs=in_specs, out_specs=out_specs, check_vma=False)
```

profile of v0, /device:TPU:0, one launch (start us, length us, event | category | flops | bytes accessed | tf_op | source)
XLA Modules:
  0.0 59.7 jit_solution(5533782162240582082)
XLA Ops:
  0.0 0.0 copy-start
  0.0 0.0 copy-start.2
  0.0 0.0 copy-start.5
  0.0 0.9 %slice.15 = bf16[2,128,256]{2,1,0:T(8,128)(2,1)S(1)} slice(bf16[2,1024,256]{2,1,0:T(8,128)(2,1)} %param.7), slice={[0:2], [896:1024], [0:256]} | slice | bytes 262144 | tf_op jit(solution)/shard_map/slice | solution.py:50
  1.0 0.0 copy-start.1
  1.0 2.4 %collective-permute-start = (bf16[2,128,256]{2,1,0:T(8,128)(2,1)S(1)}, bf16[2,128,256]{2,1,0:T(8,128)(2,1)S(1)}, u32[]{:S(2)}, u32[]{:S(2)}) collective-permute-start(bf16[2,128,256]{2,1,0:T(8,128)(2,1)S(1)} %slice.15), channel_id=1, source_target_pairs={{0,1},{2,3},{4,5},{6,7},{8,9},{10,11},{12,13},{14,15},{16,17},{18,... | collective-permute-start | bytes 393224 | tf_op jit(solution)/shard_map/ppermute | solution.py:16
  3.4 0.0 copy-done.2
  3.4 0.0 copy-done.5
  3.4 0.1 compare_and_fusion
  3.5 0.0 copy-done.1
  3.5 1.9 %all_gather.21 = bf16[2,64,256]{2,1,0:T(8,128)(2,1)S(1)} all-gather(bf16[2,32,256]{2,1,0:T(8,128)(2,1)S(1)} %copy-done.1), channel_id=1, replica_groups=mesh['user'=16,'seq'=2] {'seq'}, dimensions={1}, use_global_device_ids=true | all-gather | bytes 98304 | tf_op jit(solution)/shard_map/all_gather | solution.py:52
  5.4 2.8 %gather_fusion.1 = bf16[256,256]{1,0:T(8,128)(2,1)S(1)} fusion(bf16[2,1024,256]{2,1,0:T(8,128)(2,1)} %param.7, s32[256]{0:T(256)S(1)} %fusion.27), kind=kCustom, calls=%fused_computation.1 | custom fusion | bytes 264192 | tf_op jit(solution)/shard_map/vmap()/gather | solution.py:57
  8.2 0.0 copy-done
  8.2 0.1 fusion.2
  8.3 0.0 collective-permute-done
  8.4 1.7 %gather_fusion = bf16[256,256]{1,0:T(8,128)(2,1)S(1)} fusion(bf16[2,128,256]{2,1,0:T(8,128)(2,1)S(1)} %collective-permute-done, s32[256]{0:T(256)S(1)} %fusion.28), kind=kCustom, calls=%fused_computation | custom fusion | bytes 264192 | tf_op jit(solution)/shard_map/vmap()/gather | solution.py:57
  10.0 0.1 broadcast_select_fusion
  10.1 0.2 fusion.1
  10.3 0.4 select_reduce_fusion
  10.7 0.2 fusion.8
  10.9 0.2 fusion.6
  11.1 1.8 %all-gather.3 = f32[2,2,64]{2,1,0:T(2,128)S(1)} all-gather(f32[1,2,64]{2,1,0:T(2,128)S(1)} %bitcast.67), channel_id=3, replica_groups=mesh['user'=16,'seq'=2] {'seq'}, dimensions={0}, use_global_device_ids=true | all-gather | bytes 1536 | tf_op jit(solution)/shard_map/all_gather | solution.py:20
  12.9 1.8 %all-gather.4 = f32[2,2,64]{2,1,0:T(2,128)S(1)} all-gather(f32[1,2,64]{2,1,0:T(2,128)S(1)} %bitcast.72), channel_id=4, replica_groups=mesh['user'=16,'seq'=2] {'seq'}, dimensions={0}, use_global_device_ids=true | all-gather | bytes 1536 | tf_op jit(solution)/shard_map/all_gather | solution.py:20
  14.7 2.0 %all-gather = f32[4,64,256]{2,1,0:T(8,128)S(1)} all-gather(f32[2,64,256]{2,1,0:T(8,128)S(1)} %fusion.8), channel_id=2, replica_groups=mesh['user'=16,'seq'=2] {'seq'}, dimensions={0}, use_global_device_ids=true | all-gather | bytes 393216 | tf_op jit(solution)/shard_map/all_gather | solution.py:20
  16.7 0.1 constant_dynamic-slice_fusion.2
  16.8 0.1 constant_dynamic-slice_fusion
  16.9 0.0 copy-start.4
  16.9 0.1 fusion.30
  17.0 41.3 %all-reduce = (f32[256]{0:T(256)S(1)}, f32[256]{0:T(256)S(1)}) all-reduce(f32[256]{0:T(256)S(1)} %get-tuple-element.20, f32[256]{0:T(256)S(1)} %get-tuple-element.19), channel_id=1, replica_groups=mesh['user'=16,'seq'=2] {'user','seq'}, use_global_device_ids=true, to_apply=%region_5.6 | all-reduce | flops 512 | bytes 4096 | tf_op jit(solution)/shard_map/psum | solution.py:81
  58.4 0.0 copy-start.3
  58.4 0.0 copy-done.4
  58.4 0.7 %copy-done.3 = f32[256]{0:T(256)S(1)} copy-done((f32[256]{0:T(256)S(1)}, f32[256]{0:T(256)}, u32[]{:S(2)}) %copy-start.3) | copy-done | bytes 1048
  59.0 0.6 %add_convert_fusion = bf16[2,32,256]{2,1,0:T(8,128)(2,1)} fusion(f32[2,32,256]{2,1,0:T(8,128)S(1)} %get-tuple-element.23, f32[256]{0:T(256)S(1)} %copy-done.3, f32[256]{0:T(256)S(1)} %copy-done.4, f32[256]{0:T(256)S(1)} %get-tuple-element.40, f32[256]{0:T(256)S(1)} %get-tuple-element.39), kind=kLoop, calls=%fused_computation.15 | loop fusion | flops 81920 | bytes 102400 | tf_op jit(solution)/shard_map/convert_element_type | solution.py:88
  (9 shorter events, 0.1 us)
Async XLA Ops:
  0.0 8.2 %copy-start = (bf16[256,64]{0,1:T(8,128)(2,1)S(1)}, bf16[256,64]{0,1:T(8,128)(2,1)}, u32[]{:S(2)}) copy-start(bf16[256,64]{0,1:T(8,128)(2,1)} %param.11) | copy-start | bytes 98308
  0.0 3.4 %copy-start.2 = (s32[2,1,128]{2,1,0:T(1,128)S(1)}, s32[2,1,128]{2,1,0:T(1,128)}, u32[]{:S(2)}) copy-start(s32[2,1,128]{2,1,0:T(1,128)} %param.9) | copy-start | bytes 3076
  0.0 3.4 %copy-start.5 = (s32[2]{0:T(128)S(1)}, s32[2]{0:T(128)}, u32[]{:S(2)}) copy-start(s32[2]{0:T(128)} %param.10) | copy-start | bytes 28
  1.0 2.6 %copy-start.1 = (bf16[2,32,256]{2,1,0:T(8,128)(2,1)S(1)}, bf16[2,32,256]{2,1,0:T(8,128)(2,1)}, u32[]{:S(2)}) copy-start(bf16[2,32,256]{2,1,0:T(8,128)(2,1)} %param.8) | copy-start | bytes 98308
  1.0 7.4 %collective-permute-start = (bf16[2,128,256]{2,1,0:T(8,128)(2,1)S(1)}, bf16[2,128,256]{2,1,0:T(8,128)(2,1)S(1)}, u32[]{:S(2)}, u32[]{:S(2)}) collective-permute-start(bf16[2,128,256]{2,1,0:T(8,128)(2,1)S(1)} %slice.15), channel_id=1, source_target_pairs={{0,1},{2,3},{4,5},{6,7},{8,9},{10,11},{12,13},{14,15},{16,17},{18,... | collective-permute-start | bytes 393224 | tf_op jit(solution)/shard_map/ppermute | solution.py:16
  16.9 41.5 %copy-start.4 = (f32[256]{0:T(256)S(1)}, f32[256]{0:T(256)}, u32[]{:S(2)}) copy-start(f32[256]{0:T(256)} %param.12) | copy-start | bytes 3076
  58.4 0.7 %copy-start.3 = (f32[256]{0:T(256)S(1)}, f32[256]{0:T(256)}, u32[]{:S(2)}) copy-start(f32[256]{0:T(256)} %param.13) | copy-start | bytes 3076
where the time goes:
time: 60 us; the launch traced here: 59.7 us
  blocking collectives  48.8 us (81%)
  local copies, waits for them, and re-layouts  6.23 us (10%)
  starting transfers between devices  2.41 us (4%)
  other arithmetic  1.14 us (2%)
  matrix products  0.95 us (2%)
    psum x1, blocking collectives, shards(): lax.psum((jnp.sum(attended, axis=(0, 1)), jnp.sum(attended * attended, ax...  41.3 us
    all_gather x3, blocking collectives, joined(): everything = jax.tree.map(lambda part: lax.all_gather(part, axis), shard)  5.58 us
    gather x2, local copies, waits for them, and re-layouts, shards(): take_rows = jax.vmap(lambda row_table, where_at: row_table[where_at])  4.41 us
    ppermute x1, starting transfers between devices, passed_along(): lax.ppermute(value, axis, [(source, source + steps) for source in range(f...  2.41 us
    all_gather x1, blocking collectives, shards(): queries = lax.all_gather(candidates, 'seq', axis=1, tiled=True)  1.85 us
  transfers between devices with their start and end apart: 1, of which 0 were waited for; matrix products, arithmetic and copies ran while one was open for 5% of the time, Pallas kernels for 0%

commit v1 on v0

--- a/solution.py
+++ b/solution.py
@@ -79,7 +79,10 @@
     numerator = lax.dynamic_slice_in_dim(merged[2], seq_index * own_cands, own_cands, 1)
     attended = numerator / denominator[..., None]
     moments = lax.psum(
-        (jnp.sum(attended, axis=(0, 1)), jnp.sum(attended * attended, axis=(0, 1))), ("user", "seq")
+        lax.psum(
+            (jnp.sum(attended, axis=(0, 1)), jnp.sum(attended * attended, axis=(0, 1))), "seq"
+        ),
+        "user",
     )
     row_count = attended.shape[0] * own_cands * lax.axis_size("user") * lax.axis_size("seq")
     feature_mean = moments[0] / row_count

time: 60 us -> 64 us (1.067)
  blocking collectives: 48.8 us -> 52.8 us
    psum x0 -> x1, blocking collectives: none -> 42.8 us  [shards(): lax.psum(lax.psum((jnp.sum(attended, axis=(0, 1)), jnp.sum(attended * att...]
    psum x1, blocking collectives: 41.3 us -> 2.47 us  [shards(): lax.psum((jnp.sum(attended, axis=(0, 1)), jnp.sum(attended * attended, ax...]
where the time goes in v1:
time: 64 us; the launch traced here: 63.6 us
  blocking collectives  52.8 us (82%)
  local copies, waits for them, and re-layouts  6.24 us (10%)
  starting transfers between devices  2.41 us (4%)
  other arithmetic  1.15 us (2%)
  matrix products  0.95 us (1%)
    psum x1, blocking collectives, shards(): lax.psum(lax.psum((jnp.sum(attended, axis=(0, 1)), jnp.sum(attended * att...  42.8 us
    all_gather x3, blocking collectives, joined(): everything = jax.tree.map(lambda part: lax.all_gather(part, axis), shard)  5.58 us
    gather x2, local copies, waits for them, and re-layouts, shards(): take_rows = jax.vmap(lambda row_table, where_at: row_table[where_at])  4.41 us
    psum x1, blocking collectives, shards(): lax.psum((jnp.sum(attended, axis=(0, 1)), jnp.sum(attended * attended, ax...  2.47 us
    ppermute x1, starting transfers between devices, passed_along(): lax.ppermute(value, axis, [(source, source + steps) for source in range(f...  2.41 us
    all_gather x1, blocking collectives, shards(): queries = lax.all_gather(candidates, 'seq', axis=1, tiled=True)  1.85 us
  transfers between devices with their start and end apart: 1, of which 0 were waited for; matrix products, arithmetic and copies ran while one was open for 5% of the time, Pallas kernels for 0%

profile of v1, /device:TPU:0, one launch (start us, length us, event | category | flops | bytes accessed | tf_op | source)
XLA Modules:
  0.0 63.6 jit_solution(10260946110632408106)
XLA Ops:
  0.0 0.0 copy-start
  0.0 0.0 copy-start.2
  0.0 0.0 copy-start.5
  0.0 0.9 %slice.15 = bf16[2,128,256]{2,1,0:T(8,128)(2,1)S(1)} slice(bf16[2,1024,256]{2,1,0:T(8,128)(2,1)} %param.7), slice={[0:2], [896:1024], [0:256]} | slice | bytes 262144 | tf_op jit(solution)/shard_map/slice | solution.py:50
  1.0 0.0 copy-start.1
  1.0 2.4 %collective-permute-start = (bf16[2,128,256]{2,1,0:T(8,128)(2,1)S(1)}, bf16[2,128,256]{2,1,0:T(8,128)(2,1)S(1)}, u32[]{:S(2)}, u32[]{:S(2)}) collective-permute-start(bf16[2,128,256]{2,1,0:T(8,128)(2,1)S(1)} %slice.15), channel_id=1, source_target_pairs={{0,1},{2,3},{4,5},{6,7},{8,9},{10,11},{12,13},{14,15},{16,17},{18,... | collective-permute-start | bytes 393224 | tf_op jit(solution)/shard_map/ppermute | solution.py:16
  3.4 0.0 copy-done.2
  3.4 0.0 copy-done.5
  3.4 0.1 compare_and_fusion
  3.5 0.0 copy-done.1
  3.5 1.9 %all_gather.21 = bf16[2,64,256]{2,1,0:T(8,128)(2,1)S(1)} all-gather(bf16[2,32,256]{2,1,0:T(8,128)(2,1)S(1)} %copy-done.1), channel_id=1, replica_groups=mesh['user'=16,'seq'=2] {'seq'}, dimensions={1}, use_global_device_ids=true | all-gather | bytes 98304 | tf_op jit(solution)/shard_map/all_gather | solution.py:52
  5.4 2.8 %gather_fusion.1 = bf16[256,256]{1,0:T(8,128)(2,1)S(1)} fusion(bf16[2,1024,256]{2,1,0:T(8,128)(2,1)} %param.7, s32[256]{0:T(256)S(1)} %fusion.27), kind=kCustom, calls=%fused_computation.1 | custom fusion | bytes 264192 | tf_op jit(solution)/shard_map/vmap()/gather | solution.py:57
  8.2 0.0 copy-done
  8.2 0.1 fusion.2
  8.3 0.0 collective-permute-done
  8.4 1.7 %gather_fusion = bf16[256,256]{1,0:T(8,128)(2,1)S(1)} fusion(bf16[2,128,256]{2,1,0:T(8,128)(2,1)S(1)} %collective-permute-done, s32[256]{0:T(256)S(1)} %fusion.28), kind=kCustom, calls=%fused_computation | custom fusion | bytes 264192 | tf_op jit(solution)/shard_map/vmap()/gather | solution.py:57
  10.0 0.1 broadcast_select_fusion
  10.1 0.2 fusion.1
  10.3 0.4 select_reduce_fusion
  10.7 0.2 fusion.8
  10.9 0.2 fusion.6
  11.1 1.8 %all-gather.3 = f32[2,2,64]{2,1,0:T(2,128)S(1)} all-gather(f32[1,2,64]{2,1,0:T(2,128)S(1)} %bitcast.67), channel_id=3, replica_groups=mesh['user'=16,'seq'=2] {'seq'}, dimensions={0}, use_global_device_ids=true | all-gather | bytes 1536 | tf_op jit(solution)/shard_map/all_gather | solution.py:20
  12.9 1.8 %all-gather.4 = f32[2,2,64]{2,1,0:T(2,128)S(1)} all-gather(f32[1,2,64]{2,1,0:T(2,128)S(1)} %bitcast.72), channel_id=4, replica_groups=mesh['user'=16,'seq'=2] {'seq'}, dimensions={0}, use_global_device_ids=true | all-gather | bytes 1536 | tf_op jit(solution)/shard_map/all_gather | solution.py:20
  14.7 2.0 %all-gather = f32[4,64,256]{2,1,0:T(8,128)S(1)} all-gather(f32[2,64,256]{2,1,0:T(8,128)S(1)} %fusion.8), channel_id=2, replica_groups=mesh['user'=16,'seq'=2] {'seq'}, dimensions={0}, use_global_device_ids=true | all-gather | bytes 393216 | tf_op jit(solution)/shard_map/all_gather | solution.py:20
  16.7 0.1 constant_dynamic-slice_fusion.2
  16.8 0.1 constant_dynamic-slice_fusion
  16.9 0.0 copy-start.4
  16.9 0.1 fusion.30
  17.0 2.5 %all-reduce.1 = (f32[256]{0:T(256)S(1)}, f32[256]{0:T(256)S(1)}) all-reduce(f32[256]{0:T(256)S(1)} %get-tuple-element.20, f32[256]{0:T(256)S(1)} %get-tuple-element.19), channel_id=1, replica_groups=mesh['user'=16,'seq'=2] {'seq'}, use_global_device_ids=true, to_apply=%region_6.7 | all-reduce | flops 512 | bytes 4096 | tf_op jit(solution)/shard_map/psum | solution.py:82
  19.5 42.8 %all-reduce = (f32[256]{0:T(256)S(1)}, f32[256]{0:T(256)S(1)}) all-reduce(f32[256]{0:T(256)S(1)} %get-tuple-element.23, f32[256]{0:T(256)S(1)} %get-tuple-element.32), channel_id=1, replica_groups=mesh['user'=16,'seq'=2] {'user'}, use_global_device_ids=true, to_apply=%region_7.8 | all-reduce | flops 512 | bytes 4096 | tf_op jit(solution)/shard_map/psum | solution.py:81
  62.3 0.0 copy-start.3
  62.3 0.0 copy-done.4
  62.3 0.7 %copy-done.3 = f32[256]{0:T(256)S(1)} copy-done((f32[256]{0:T(256)S(1)}, f32[256]{0:T(256)}, u32[]{:S(2)}) %copy-start.3) | copy-done | bytes 1048
  63.0 0.6 add_convert_fusion
  (9 shorter events, 0.1 us)
Async XLA Ops:
  0.0 8.2 %copy-start = (bf16[256,64]{0,1:T(8,128)(2,1)S(1)}, bf16[256,64]{0,1:T(8,128)(2,1)}, u32[]{:S(2)}) copy-start(bf16[256,64]{0,1:T(8,128)(2,1)} %param.11) | copy-start | bytes 98308
  0.0 3.4 %copy-start.2 = (s32[2,1,128]{2,1,0:T(1,128)S(1)}, s32[2,1,128]{2,1,0:T(1,128)}, u32[]{:S(2)}) copy-start(s32[2,1,128]{2,1,0:T(1,128)} %param.9) | copy-start | bytes 3076
  0.0 3.4 %copy-start.5 = (s32[2]{0:T(128)S(1)}, s32[2]{0:T(128)}, u32[]{:S(2)}) copy-start(s32[2]{0:T(128)} %param.10) | copy-start | bytes 28
  1.0 2.6 %copy-start.1 = (bf16[2,32,256]{2,1,0:T(8,128)(2,1)S(1)}, bf16[2,32,256]{2,1,0:T(8,128)(2,1)}, u32[]{:S(2)}) copy-start(bf16[2,32,256]{2,1,0:T(8,128)(2,1)} %param.8) | copy-start | bytes 98308
  1.0 7.4 %collective-permute-start = (bf16[2,128,256]{2,1,0:T(8,128)(2,1)S(1)}, bf16[2,128,256]{2,1,0:T(8,128)(2,1)S(1)}, u32[]{:S(2)}, u32[]{:S(2)}) collective-permute-start(bf16[2,128,256]{2,1,0:T(8,128)(2,1)S(1)} %slice.15), channel_id=1, source_target_pairs={{0,1},{2,3},{4,5},{6,7},{8,9},{10,11},{12,13},{14,15},{16,17},{18,... | collective-permute-start | bytes 393224 | tf_op jit(solution)/shard_map/ppermute | solution.py:16
  16.9 45.4 %copy-start.4 = (f32[256]{0:T(256)S(1)}, f32[256]{0:T(256)}, u32[]{:S(2)}) copy-start(f32[256]{0:T(256)} %param.12) | copy-start | bytes 3076
  62.3 0.7 %copy-start.3 = (f32[256]{0:T(256)S(1)}, f32[256]{0:T(256)}, u32[]{:S(2)}) copy-start(f32[256]{0:T(256)} %param.13) | copy-start | bytes 3076
